TPU v7x, 32 devices: a whole 2x2x4 slice. The times are simulated.
32 devices in a mesh: groups: 2 (over x), wide: 16 (over z, y, core).
Axes of the slice: x: 2, y: 2, z: 4, core: 2. Of those that a mesh axis runs over, the one named last changes fastest.
Arguments:
- half_integrals: float32 [256, 512, 800], P(('groups', 'wide')), parts along dimension 0, may hold values from -40 to 40
- pair_list: int32 [256, 2], P('groups'), parts along dimension 0, may hold values from 0 to 199, as said below
- occupied_energy: float32 [400], P('groups'), parts along dimension 0, may hold values from -3 to -0.3
- virtual_orbitals: float32 [1600, 600], P('groups'), parts along dimension 0, may hold values from -0.21875 to 0.21875
- tile_order: int32 [64], replicated, may hold values from 0 to 63, each once
Outputs:
- transformed: float32 [256, 512, 600], P('groups', 'wide'), parts along dimension 0
- pair_rms: float32 [256], P('groups'), parts along dimension 0
There are 2 independent parts, one for each index of `groups`. A program takes and returns all parts, laid end to end along the dimension named above; an argument that names none is the same for every part. Nothing has to cross between parts.
Inputs may be any that keep to these rules, and one draw needn't show every extreme that they name: `pair_list`: each row is a distinct pair (i, j) with i <= j.
All inputs are finite; a program needn't handle non-finite values.
Results may differ from a plain program's by a relative error of at most 0.00007.
Values sent between devices are 32-bit elements; how exact they have to be, the bound alone decides.
A program may use at most 128 MiB of HBM per device.

v0:
```python
import functools

import jax
import jax.numpy as jnp
from jax import lax
from jax.experimental import pallas as pl
from jax.experimental.pallas import tpu as pltpu
from jax.sharding import PartitionSpec as P

TILE_S = 8
LANES = 128
MESH = pl.DeviceIdType.MESH


def round_up(value, step):
    return (value + step - 1) // step * step


def split(value):
    high = value.astype(jnp.bfloat16)
    low = (value - high.astype(jnp.float32)).astype(jnp.bfloat16)
    return high, low


def prepare_kernel(
    order_ref, pair_ref, energy_ref, x_ref, w_ref, xs, w_high, w_low, scales,
    index_buf, turned, slot_of, sems,
):
    me = lax.axis_index("wide")
    step = pl.program_id(0)
    steps = pl.num_programs(0)
    pair_rows, basis, _ = x_ref.shape
    virtuals = w_ref.shape[1]
    deep = xs.shape[0]
    block_rows = TILE_S * pair_rows
    tiles = LANES // TILE_S
    side = lax.rem(step, 2)

    @pl.when(step == 0)
    def _():
        def invert(k, carry):
            slot_of[order_ref[k]] = k
            return carry

        lax.fori_loop(0, order_ref.shape[0], invert, 0)
        w_high[...] = jnp.zeros_like(w_high)
        w_low[...] = jnp.zeros_like(w_low)
        high, low = split(w_ref[...])
        w_high[:basis, :virtuals] = high
        w_low[:basis, :virtuals] = low
        my_rows = pl.ds(pl.multiple_of(me * pair_rows, pair_rows), pair_rows)
        orbitals = energy_ref.shape[1]
        orbital = lax.broadcasted_iota(jnp.int32, (pair_rows, orbitals), 1).astype(jnp.float32)
        energy = jnp.zeros((pair_rows, 1), jnp.float32)
        for k in range(2):
            line = pair_ref[k : k + 1, :].astype(jnp.float32)
            index_buf[...] = jnp.broadcast_to(line, (LANES, line.shape[1])).T
            hit = index_buf[my_rows, 0:1] == orbital
            energy = energy + jnp.sum(jnp.where(hit, energy_ref[...], 0.0), axis=1, keepdims=True)
        scales[...] = jnp.broadcast_to(jnp.exp(0.3 * energy), scales.shape)

    def copy(at, which, u):
        rows = pl.ds(pl.multiple_of(slot_of[at * tiles + u] * block_rows, block_rows), block_rows)
        return pltpu.make_async_copy(
            turned.at[which, :, pl.ds(u * block_rows, block_rows), :], xs.at[:, rows, :], sems.at[which, u]
        )

    @pl.when(step >= 2)
    def _():
        for u in range(tiles):
            copy(step - 2, side, u).wait()

    for p in range(pair_rows):
        for k in range(deep):
            size = min(LANES, basis - k * LANES)
            piece = x_ref[p, k * LANES : k * LANES + size, :]
            if size < LANES:
                piece = jnp.concatenate([piece, jnp.zeros((LANES - size, LANES), jnp.float32)], axis=0)
            turned[side, k, pl.ds(p, LANES, stride=pair_rows), :] = piece.T
    for u in range(tiles):
        copy(step, side, u).start()

    @pl.when(step == steps - 1)
    def _():
        for u in range(tiles):
            copy(step - 1, 1 - side, u).wait()
        for u in range(tiles):
            copy(step, side, u).wait()


def exchange_kernel(
    n, xs, w_high, w_low, scales, recv_main, recv_rest, sq_recv,
    x_buf, x_high, x_low, squares, sq_send, send_main, send_rest,
    x_sems, main_sems, rest_sems, main_recv_sems, rest_recv_sems,
    sq_sems, sq_recv_sems, own_sems,
):
    me = lax.axis_index("wide")
    _, span, pair_rows, full = send_main.shape
    rest = send_rest.shape[2] // span
    rows = span * pair_rows
    deep = xs.shape[0]
    plane = n // 4
    my_rows = pl.ds(pl.multiple_of(me * pair_rows, pair_rows), pair_rows)

    barrier = pltpu.get_barrier_semaphore()

    def greet(j, carry):
        pl.semaphore_signal(barrier, inc=1, device_id={"wide": lax.rem(me + j, n)}, device_id_type=MESH)
        return carry

    lax.fori_loop(1, n, greet, 0)

    sign = 1 - 2 * (me // (n // 2))
    my_plane = me // plane

    def place(c):
        other = lax.rem(my_plane + sign * (1 + c // plane) + 8, 4)
        return other * plane + lax.rem(me + c, plane)

    def fetch(c):
        source = pl.ds(pl.multiple_of(place(c) * rows, rows), rows)
        side = lax.rem(c, 2)
        return pltpu.make_async_copy(xs.at[:, source, :], x_buf.at[side], x_sems.at[side])

    fetch(0).start()
    squares[...] = jnp.zeros_like(squares)

    def remotes(c, owner):
        return (
            pltpu.make_async_remote_copy(
                src_ref=send_main.at[c], dst_ref=recv_main.at[:, my_rows, :],
                send_sem=main_sems.at[c], recv_sem=main_recv_sems.at[me],
                device_id={"wide": owner}, device_id_type=MESH,
            ),
            pltpu.make_async_remote_copy(
                src_ref=send_rest.at[c], dst_ref=recv_rest.at[my_rows, :],
                send_sem=rest_sems.at[c], recv_sem=rest_recv_sems.at[me],
                device_id={"wide": owner}, device_id_type=MESH,
            ),
        )

    def locals_(c):
        return (
            pltpu.make_async_copy(send_main.at[c], recv_main.at[:, my_rows, :], own_sems.at[0]),
            pltpu.make_async_copy(send_rest.at[c], recv_rest.at[my_rows, :], own_sems.at[1]),
        )

    def dispatch(c):
        owner = place(c)

        @pl.when(owner != me)
        def _():
            for copy in remotes(c, owner):
                copy.start()

        @pl.when(owner == me)
        def _():
            for copy in locals_(c):
                copy.start()

    lane = lax.broadcasted_iota(jnp.int32, (pair_rows, LANES), 1)

    def block(c, carry):
        @pl.when(c + 1 < n)
        def _():
            fetch(c + 1).start()

        fetch(c).wait()
        for k in range(deep):
            high, low = split(x_buf[lax.rem(c, 2), k])
            x_high[:, k * LANES : (k + 1) * LANES] = high
            x_low[:, k * LANES : (k + 1) * LANES] = low

        @pl.when(c == 1)
        def _():
            pl.semaphore_wait(barrier, n - 1)

        @pl.when(c > 0)
        def _():
            dispatch(c - 1)

        dot = functools.partial(jnp.dot, preferred_element_type=jnp.float32)
        small = dot(x_low[...], w_high[...]) + dot(x_high[...], w_low[...])
        product = (dot(x_high[...], w_high[...]) + small).reshape(span, pair_rows, -1) * scales[...][None]
        squares[...] = squares[...] + jnp.sum(product * product, axis=0)
        send_main[c] = product[:, :, :full]
        packed = [jnp.zeros((pair_rows, LANES), jnp.float32)] * (span * rest // LANES)
        for s in range(span):
            at, offset = divmod(s * rest, LANES)
            value = product[s, :, full:]
            if offset:
                value = pltpu.roll(value, offset, axis=1)
            if offset + rest > LANES:
                packed[at] = jnp.where(lane >= offset, value, packed[at])
                packed[at + 1] = jnp.where(lane < offset, value, packed[at + 1])
            else:
                packed[at] = jnp.where(lane >= offset, value, packed[at])
        for b, value in enumerate(packed):
            send_rest[c, :, b * LANES : (b + 1) * LANES] = value

        return carry

    lax.fori_loop(0, n, block, 0)
    dispatch(n - 1)
    total = squares[:, :LANES]
    for b in range(1, squares.shape[1] // LANES):
        total = total + squares[:, b * LANES : (b + 1) * LANES]
    sq_send[...] = total

    def sq_copy(src, dst, j):
        return pltpu.make_async_remote_copy(
            src_ref=sq_send, dst_ref=sq_recv.at[src],
            send_sem=sq_sems.at[j], recv_sem=sq_recv_sems.at[src],
            device_id={"wide": dst}, device_id_type=MESH,
        )

    for copy in remotes(0, place(0)):
        copy.wait_send()
    own_squares = pltpu.make_async_copy(sq_send, sq_recv.at[me], own_sems.at[2])
    own_squares.start()

    def send_squares(j, carry):
        sq_copy(me, lax.rem(me + j, n), j).start()
        return carry

    lax.fori_loop(1, n, send_squares, 0)
    own_squares.wait()

    def finish_sends(c, carry):
        owner = place(c)

        @pl.when(owner != me)
        def _():
            for copy in remotes(c, owner):
                copy.wait_send()

        @pl.when(owner == me)
        def _():
            for copy in locals_(c):
                copy.wait()

        return carry

    lax.fori_loop(1, n, finish_sends, 0)

    def finish(j, carry):
        src = lax.rem(me + j, n)
        rows = pl.ds(pl.multiple_of(src * pair_rows, pair_rows), pair_rows)
        pltpu.make_async_remote_copy(
            src_ref=send_main.at[0], dst_ref=recv_main.at[:, rows, :],
            send_sem=main_sems.at[0], recv_sem=main_recv_sems.at[src],
            device_id={"wide": src}, device_id_type=MESH,
        ).wait_recv()
        pltpu.make_async_remote_copy(
            src_ref=send_rest.at[0], dst_ref=recv_rest.at[rows, :],
            send_sem=rest_sems.at[0], recv_sem=rest_recv_sems.at[src],
            device_id={"wide": src}, device_id_type=MESH,
        ).wait_recv()
        sq_copy(src, src, j).wait_recv()
        sq_copy(me, src, j).wait_send()
        return carry

    lax.fori_loop(1, n, finish, 0)


def unpack_kernel(count, main_ref, rest_ref, sq_ref, out_ref, rms_ref, turned):
    group, pairs, full = main_ref.shape
    rest = out_ref.shape[1] - full
    step = pl.program_id(0)

    @pl.when(step == 0)
    def _():
        for b in range(rest_ref.shape[1] // LANES):
            turned[b * LANES : (b + 1) * LANES, :] = rest_ref[:, b * LANES : (b + 1) * LANES].T
        totals = jnp.sum(sq_ref[...].T, axis=0, keepdims=True)
        rms_ref[...] = jnp.sqrt(totals / count + 1e-06)

    for g in range(group):
        for b in range(full // LANES):
            out_ref[g, b * LANES : (b + 1) * LANES, :] = main_ref[g, :, b * LANES : (b + 1) * LANES].T
        start = pl.multiple_of((step * group + g) * rest, 8)
        out_ref[g, full:, :] = turned[pl.ds(start, rest), :]


def shards(n, half_integrals, pair_list, occupied_energy, virtual_orbitals, tile_order):
    pair_rows, columns, basis = half_integrals.shape
    virtuals = virtual_orbitals.shape[1]
    pairs = n * pair_rows
    span = columns // n
    deep = round_up(basis, LANES)
    broad = round_up(virtuals, LANES)
    full = virtuals // LANES * LANES
    rest = virtuals - full
    rows = span * pair_rows
    group = 4
    flops = 6 * pair_rows * columns * basis * virtuals
    vmem = pl.BlockSpec(memory_space=pltpu.VMEM)
    anywhere = pl.BlockSpec(memory_space=pl.ANY)

    def whole(*shape):
        return pl.BlockSpec(shape, lambda i: (0,) * len(shape))

    tiles = LANES // TILE_S
    xs, w_high, w_low, scales = pl.pallas_call(
        prepare_kernel,
        grid=(columns // LANES,),
        out_shape=(
            jax.ShapeDtypeStruct((deep // LANES, columns * pair_rows, LANES), jnp.float32),
            jax.ShapeDtypeStruct((deep, broad), jnp.bfloat16),
            jax.ShapeDtypeStruct((deep, broad), jnp.bfloat16),
            jax.ShapeDtypeStruct((pair_rows, broad), jnp.float32),
        ),
        in_specs=[
            pl.BlockSpec(memory_space=pltpu.SMEM),
            whole(2, pairs),
            whole(1, occupied_energy.shape[0]),
            pl.BlockSpec((pair_rows, basis, LANES), lambda i: (0, 0, i)),
            whole(basis, virtuals),
        ],
        out_specs=(anywhere, whole(deep, broad), whole(deep, broad), whole(pair_rows, broad)),
        scratch_shapes=[
            pltpu.VMEM((pairs, LANES), jnp.float32),
            pltpu.VMEM((2, deep // LANES, LANES * pair_rows, LANES), jnp.float32),
            pltpu.SMEM(tile_order.shape, jnp.int32),
            pltpu.SemaphoreType.DMA((2, tiles)),
        ],
        compiler_params=pltpu.CompilerParams(vmem_limit_bytes=28 * 1024 * 1024),
        name="prepare",
    )(tile_order, pair_list.T, occupied_energy.reshape(1, -1), pltpu.with_memory_space_constraint(jnp.swapaxes(half_integrals, 1, 2), pltpu.HBM), virtual_orbitals)
    recv_main, recv_rest, sq_recv = pl.pallas_call(
        functools.partial(exchange_kernel, n),
        out_shape=(
            jax.ShapeDtypeStruct((span, pairs, full), jnp.float32),
            jax.ShapeDtypeStruct((pairs, span * rest), jnp.float32),
            jax.ShapeDtypeStruct((n, pair_rows, LANES), jnp.float32),
        ),
        in_specs=[anywhere, vmem, vmem, vmem],
        out_specs=(anywhere, anywhere, anywhere),
        scratch_shapes=[
            pltpu.VMEM((2, deep // LANES, rows, LANES), jnp.float32),
            pltpu.VMEM((rows, deep), jnp.bfloat16),
            pltpu.VMEM((rows, deep), jnp.bfloat16),
            pltpu.VMEM((pair_rows, broad), jnp.float32),
            pltpu.VMEM((pair_rows, LANES), jnp.float32),
            pltpu.VMEM((n, span, pair_rows, full), jnp.float32),
            pltpu.VMEM((n, pair_rows, span * rest), jnp.float32),
            pltpu.SemaphoreType.DMA((2,)),
            pltpu.SemaphoreType.DMA((n,)),
            pltpu.SemaphoreType.DMA((n,)),
            pltpu.SemaphoreType.DMA((n,)),
            pltpu.SemaphoreType.DMA((n,)),
            pltpu.SemaphoreType.DMA((n,)),
            pltpu.SemaphoreType.DMA((n,)),
            pltpu.SemaphoreType.DMA((3,)),
        ],
        compiler_params=pltpu.CompilerParams(
            collective_id=0, has_side_effects=True, vmem_limit_bytes=20 * 1024 * 1024
        ),
        cost_estimate=pl.CostEstimate(flops=flops, bytes_accessed=4 * half_integrals.size, transcendentals=0),
        name="exchange",
    )(xs, w_high, w_low, scales)
    out, rms = pl.pallas_call(
        functools.partial(unpack_kernel, columns * virtuals),
        grid=(span // group,),
        out_shape=(
            jax.ShapeDtypeStruct((span, virtuals, pairs), jnp.float32),
            jax.ShapeDtypeStruct((1, pairs), jnp.float32),
        ),
        in_specs=[
            pl.BlockSpec((group, pairs, full), lambda i: (i, 0, 0)),
            pl.BlockSpec((pairs, span * rest), lambda i: (0, 0)),
            pl.BlockSpec((pairs, LANES), lambda i: (0, 0)),
        ],
        out_specs=(
            pl.BlockSpec((group, virtuals, pairs), lambda i: (i, 0, 0)),
            pl.BlockSpec((1, pairs), lambda i: (0, 0)),
        ),
        scratch_shapes=[pltpu.VMEM((span * rest, pairs), jnp.float32)],
        compiler_params=pltpu.CompilerParams(vmem_limit_bytes=20 * 1024 * 1024),
        name="unpack",
    )(recv_main, recv_rest, sq_recv.reshape(pairs, LANES))
    return (jnp.transpose(out, (2, 0, 1)), rms.reshape(-1))


def solution(mesh):
    in_specs = (
        P(("groups", "wide"), None, None),
        P("groups", None),
        P("groups"),
        P("groups", None),
        P(),
    )
    out_specs = (P("groups", "wide", None), P("groups"))
    return jax.shard_map(
        functools.partial(shards, mesh.shape["wide"]),
        mesh=mesh, in_specs=in_specs, out_specs=out_specs, check_vma=False,
    )
```

profile of v0, /device:TPU:9, one launch (start us, length us, event | category | flops | bytes accessed | tf_op | source)
XLA Modules:
  0.0 251.8 jit_solution(15625946934485084664)
XLA Ops:
  0.6 0.0 copy-start
  0.6 1.6 copy-done
  2.2 0.0 copy-start.1
  2.2 0.7 copy-done.1
  2.9 0.0 copy-start.2
  2.9 0.7 copy-done.2
  3.6 0.0 copy-start.3
  3.6 0.7 copy-done.3
  4.2 11.7 %prepare.1 = (f32[7,4096,128]{2,1,0:T(8,128)S(1)}, bf16[896,640]{1,0:T(8,128)(2,1)S(1)}, bf16[896,640]{1,0:T(8,128)(2,1)S(1)}, f32[8,640]{1,0:T(8,128)S(1)}) custom-call(s32[64]{0:T(128)S(1)} %copy-done.3, s32[2,128]{1,0:T(2,128)S(1)} %bitcast.7, f32[1,200]{1,0:T(1,128)S(1)} %bitcast.8, f32[8,800,512]{2,1,0:T(8,128)} %bitcast.9, f32[800,600]{1,0:T(8,128)S(1)} %copy-done), custom_call_target="tpu_custom_call" | custom-call | tf_op jit(solution)/shard_map/prepare/pallas_call | solution.py:304
  15.9 229.6 %exchange.1 = (f32[32,128,512]{2,1,0:T(8,128)S(1)}, f32[128,2816]{1,0:T(8,128)S(1)}, f32[16,8,128]{2,1,0:T(8,128)S(1)}) custom-call(f32[7,4096,128]{2,1,0:T(8,128)S(1)} %get-tuple-element.11.xs, bf16[896,640]{1,0:T(8,128)(2,1)S(1)} %get-tuple-element.12.w_high, bf16[896,640]{1,0:T(8,128)(2,1)S(1)} %get-tuple-element.13.w_low, ...), custom_call_target="tpu_custom_call" | custom-call | flops 11796480000 | bytes 13107200 | tf_op jit(solution)/shard_map/exchange/pallas_call | solution.py:330
  245.5 6.4 %unpack.1 = (f32[32,600,128]{2,1,0:T(8,128)}, f32[1,128]{1,0:T(1,128)}) custom-call(f32[32,128,512]{2,1,0:T(8,128)S(1)} %get-tuple-element.15.main_ref, f32[128,2816]{1,0:T(8,128)S(1)} %get-tuple-element.16.rest_ref, f32[128,128]{1,0:T(8,128)S(1)} %bitcast.6), custom_call_target="tpu_custom_call" | custom-call | tf_op jit(solution)/shard_map/unpack/pallas_call | solution.py:362
Async XLA Ops:
  0.6 1.6 copy-start
  2.2 0.7 copy-start.1
  2.9 0.7 copy-start.2
  3.6 0.7 copy-start.3
where the time goes:
time: 254 us; the launch traced here: 252 us
  Pallas kernels  248 us (98%)
  local copies, waits for them, and re-layouts  3.58 us (1%)
    pallas_call x1, Pallas kernels, shards(): pl.pallas_call(functools.partial(exchange_kernel, n), out_shape=(jax.Shap...  230 us
    pallas_call x1, Pallas kernels, shards(): pl.pallas_call(prepare_kernel, grid=(columns // LANES,), out_shape=(jax.S...  11.7 us
    pallas_call x1, Pallas kernels, shards(): pl.pallas_call(functools.partial(unpack_kernel, columns * virtuals), grid...  6.36 us

commit v1 on v0

--- a/solution.py
+++ b/solution.py
@@ -112,10 +112,12 @@
 
     sign = 1 - 2 * (me // (n // 2))
     my_plane = me // plane
+    inner = jnp.minimum(my_plane, 3 - my_plane)
 
     def place(c):
-        other = lax.rem(my_plane + sign * (1 + c // plane) + 8, 4)
-        return other * plane + lax.rem(me + c, plane)
+        rank = c // plane
+        away = 3 - rank - inner * jnp.where(rank < 2, 1, 6 - 2 * rank)
+        return (my_plane + sign * away) * plane + lax.rem(me + c, plane)
 
     def fetch(c):
         source = pl.ds(pl.multiple_of(place(c) * rows, rows), rows)

time: 254 us -> 243 us (0.957)
  Pallas kernels: 248 us -> 237 us
    pallas_call x1, Pallas kernels: 230 us -> 219 us  [shards(): pl.pallas_call(functools.partial(exchange_kernel, n), out_shape=(jax.Shap...]
where the time goes in v1:
time: 243 us; the launch traced here: 241 us
  Pallas kernels  237 us (98%)
  local copies, waits for them, and re-layouts  3.58 us (1%)
    pallas_call x1, Pallas kernels, shards(): pl.pallas_call(functools.partial(exchange_kernel, n), out_shape=(jax.Shap...  219 us
    pallas_call x1, Pallas kernels, shards(): pl.pallas_call(prepare_kernel, grid=(columns // LANES,), out_shape=(jax.S...  11.7 us
    pallas_call x1, Pallas kernels, shards(): pl.pallas_call(functools.partial(unpack_kernel, columns * virtuals), grid...  6.36 us

profile of v1, /device:TPU:9, one launch (start us, length us, event | category | flops | bytes accessed | tf_op | source)
XLA Modules:
  0.0 241.3 jit_solution(18226763817443039622)
XLA Ops:
  0.6 0.0 copy-start
  0.6 1.6 copy-done
  2.2 0.0 copy-start.1
  2.2 0.7 copy-done.1
  2.9 0.0 copy-start.2
  2.9 0.7 copy-done.2
  3.6 0.0 copy-start.3
  3.6 0.7 copy-done.3
  4.2 11.7 %prepare.1 = (f32[7,4096,128]{2,1,0:T(8,128)S(1)}, bf16[896,640]{1,0:T(8,128)(2,1)S(1)}, bf16[896,640]{1,0:T(8,128)(2,1)S(1)}, f32[8,640]{1,0:T(8,128)S(1)}) custom-call(s32[64]{0:T(128)S(1)} %copy-done.3, s32[2,128]{1,0:T(2,128)S(1)} %bitcast.7, f32[1,200]{1,0:T(1,128)S(1)} %bitcast.8, f32[8,800,512]{2,1,0:T(8,128)} %bitcast.9, f32[800,600]{1,0:T(8,128)S(1)} %copy-done), custom_call_target="tpu_custom_call" | custom-call | tf_op jit(solution)/shard_map/prepare/pallas_call | solution.py:306
  15.9 219.0 %exchange.1 = (f32[32,128,512]{2,1,0:T(8,128)S(1)}, f32[128,2816]{1,0:T(8,128)S(1)}, f32[16,8,128]{2,1,0:T(8,128)S(1)}) custom-call(f32[7,4096,128]{2,1,0:T(8,128)S(1)} %get-tuple-element.11.xs, bf16[896,640]{1,0:T(8,128)(2,1)S(1)} %get-tuple-element.12.w_high, bf16[896,640]{1,0:T(8,128)(2,1)S(1)} %get-tuple-element.13.w_low, ...), custom_call_target="tpu_custom_call" | custom-call | flops 11796480000 | bytes 13107200 | tf_op jit(solution)/shard_map/exchange/pallas_call | solution.py:332
  234.9 6.4 %unpack.1 = (f32[32,600,128]{2,1,0:T(8,128)}, f32[1,128]{1,0:T(1,128)}) custom-call(f32[32,128,512]{2,1,0:T(8,128)S(1)} %get-tuple-element.15.main_ref, f32[128,2816]{1,0:T(8,128)S(1)} %get-tuple-element.16.rest_ref, f32[128,128]{1,0:T(8,128)S(1)} %bitcast.6), custom_call_target="tpu_custom_call" | custom-call | tf_op jit(solution)/shard_map/unpack/pallas_call | solution.py:364
Async XLA Ops:
  0.6 1.6 copy-start
  2.2 0.7 copy-start.1
  2.9 0.7 copy-start.2
  3.6 0.7 copy-start.3

commit v2 on v1

v2 whole, which is shorter than its diff:
```python
import functools
import math

import jax
import jax.numpy as jnp
from jax import lax
from jax.experimental import pallas as pl
from jax.experimental.pallas import tpu as pltpu
from jax.sharding import PartitionSpec as P

TILE_S = 8
LANES = 128
EARLY = 2
MESH = pl.DeviceIdType.MESH


def round_up(value, step):
    return (value + step - 1) // step * step


def split(value):
    high = value.astype(jnp.bfloat16)
    low = (value - high.astype(jnp.float32)).astype(jnp.bfloat16)
    return high, low


def schedule(span, rest):
    wide = LANES // math.gcd(rest, LANES)
    sets = [("pair", p) for p in range(EARLY)]
    for g in range(span // wide):
        sets.append(("rest", g))
        sets += [("main", g * wide // TILE_S + k) for k in range(wide // TILE_S)]
    return wide, sets


def exchange_kernel(
    n, rest, order_hbm, pair_hbm, energy_hbm, x_hbm, w_hbm, out_ref, sq_recv,
    order_ref, pair_ref, energy_ref, index_buf, w_buf, x_buf, turned, x_high, x_low, w_high, w_low, scales, squares,
    send_main, rest_rows, send_rest, sq_send, recv_main, recv_rest, rest_turned,
    small_sems, w_sem, x_sems, send_sems, recv_sems, sq_sems, sq_recv_sems,
):
    me = lax.axis_index("wide")
    pair_rows, basis, columns = x_hbm.shape
    virtuals = w_hbm.shape[1]
    span, _, pairs = out_ref.shape
    full = virtuals - rest
    deep = turned.shape[1]
    groups = full // LANES
    plane = n // 4
    half = n // 2
    rows = half * span
    own = 3 * plane
    owner_tiles = span // TILE_S
    stride = recv_main.shape[2]
    wide, sets = schedule(span, rest)
    late = pair_rows - EARLY
    my_pair = pl.multiple_of(me * pair_rows, pair_rows)

    barrier = pltpu.get_barrier_semaphore()

    def greet(j, carry):
        pl.semaphore_signal(barrier, inc=1, device_id={"wide": lax.rem(me + j, n)}, device_id_type=MESH)
        return carry

    small = [
        pltpu.make_async_copy(order_hbm, order_ref, small_sems.at[0]),
        pltpu.make_async_copy(pair_hbm, pair_ref, small_sems.at[1]),
        pltpu.make_async_copy(energy_hbm, energy_ref, small_sems.at[2]),
    ]
    weights_copy = pltpu.make_async_copy(w_hbm, w_buf, w_sem.at[0])

    def fetch(p):
        return pltpu.make_async_copy(x_hbm.at[p], x_buf.at[p], x_sems.at[p])

    weights_copy.start()
    fetch(0).start()
    for copy in small:
        copy.start()
    for p in range(1, pair_rows):
        fetch(p).start()
    lax.fori_loop(1, n, greet, 0)

    sign = 1 - 2 * (me // half)
    my_plane = me // plane
    inner = jnp.minimum(my_plane, 3 - my_plane)

    def place(c):
        rank = c // plane
        away = 3 - rank - inner * jnp.where(rank < 2, 1, 6 - 2 * rank)
        return (my_plane + sign * away) * plane + lax.rem(me + c, plane)

    squares[...] = jnp.zeros_like(squares)
    w_high[...] = jnp.zeros_like(w_high)
    w_low[...] = jnp.zeros_like(w_low)
    for copy in small:
        copy.wait()
    orbitals = energy_ref.shape[1]
    orbital = lax.broadcasted_iota(jnp.int32, (pair_rows, orbitals), 1).astype(jnp.float32)
    energy = jnp.zeros((pair_rows, 1), jnp.float32)
    for k in range(2):
        line = pair_ref[k : k + 1, :].astype(jnp.float32)
        index_buf[...] = jnp.broadcast_to(line, (LANES, pairs)).T
        hit = index_buf[pl.ds(my_pair, pair_rows), 0:1] == orbital
        energy = energy + jnp.sum(jnp.where(hit, energy_ref[...], 0.0), axis=1, keepdims=True)
    scales[...] = jnp.broadcast_to(jnp.exp(0.3 * energy), scales.shape)
    weights_copy.wait()
    high, low = split(w_buf[...])
    w_high[:basis, :virtuals] = high
    w_low[:basis, :virtuals] = low

    def remote(i, c, owner):
        kind, at = sets[i]
        if kind == "pair":
            src = send_main.at[c, :, at, :, :]
            dst = recv_main.at[:, my_pair + at, pl.ds(0, span), :]
        elif kind == "main":
            src = send_main.at[c, :, pl.ds(EARLY, late), pl.ds(at * TILE_S, TILE_S), :]
            dst = recv_main.at[:, pl.ds(my_pair + EARLY, late), pl.ds(at * TILE_S, TILE_S), :]
        else:
            lanes = pl.ds(at * wide * rest, wide * rest)
            src = send_rest.at[c, :, lanes]
            dst = recv_rest.at[pl.ds(my_pair, pair_rows), lanes]
        return pltpu.make_async_remote_copy(
            src_ref=src, dst_ref=dst, send_sem=send_sems.at[i, c], recv_sem=recv_sems.at[i, me],
            device_id={"wide": owner}, device_id_type=MESH,
        )

    def arrival(i, src):
        kind, at = sets[i]
        first = pl.multiple_of(src * pair_rows, pair_rows)
        if kind == "pair":
            local = send_main.at[0, :, at, :, :]
            dst = recv_main.at[:, first + at, pl.ds(0, span), :]
        elif kind == "main":
            local = send_main.at[0, :, pl.ds(EARLY, late), pl.ds(at * TILE_S, TILE_S), :]
            dst = recv_main.at[:, pl.ds(first + EARLY, late), pl.ds(at * TILE_S, TILE_S), :]
        else:
            lanes = pl.ds(at * wide * rest, wide * rest)
            local = send_rest.at[0, :, lanes]
            dst = recv_rest.at[pl.ds(first, pair_rows), lanes]
        return pltpu.make_async_remote_copy(
            src_ref=local, dst_ref=dst, send_sem=send_sems.at[i, 0], recv_sem=recv_sems.at[i, src],
            device_id={"wide": src}, device_id_type=MESH,
        )

    def send(i, first, last):
        def one(c, carry):
            remote(i, c, place(c)).start()
            return carry

        lax.fori_loop(first, min(last, own), one, 0)
        lax.fori_loop(max(first, own + 1), last, one, 0)

    def compute(step, carry):
        p = step // 2
        part = lax.rem(step, 2)

        @pl.when(part == 0)
        def _():
            fetch(p).wait()
            for k in range(deep // LANES):
                size = min(LANES, basis - k * LANES)
                for b in range(columns // LANES):
                    piece = x_buf[p, k * LANES : k * LANES + size, b * LANES : (b + 1) * LANES]
                    if size < LANES:
                        piece = jnp.concatenate([piece, jnp.zeros((LANES - size, LANES), jnp.float32)], axis=0)
                    turned[b * LANES : (b + 1) * LANES, k * LANES : (k + 1) * LANES] = piece.T

        def gather(u, carry):
            pieces = []
            for v in range(2):
                at = u * 2 + v
                slot = place(part * half + at // owner_tiles) * owner_tiles + lax.rem(at, owner_tiles)
                pieces.append(turned[pl.ds(order_ref[slot] * TILE_S, TILE_S), :])
            high, low = split(jnp.concatenate(pieces, axis=0))
            block = pl.ds(pl.multiple_of(u * 2 * TILE_S, 2 * TILE_S), 2 * TILE_S)
            x_high[block, :] = high
            x_low[block, :] = low
            return carry

        lax.fori_loop(0, rows // TILE_S // 2, gather, 0, unroll=2)
        dot = functools.partial(jnp.dot, preferred_element_type=jnp.float32)
        small = dot(x_low[...], w_high[...]) + dot(x_high[...], w_low[...])
        product = dot(x_high[...], w_high[...]) + small
        scale = scales[pl.ds(p, 1), :]
        total = squares[p]
        first = part * half
        for b in range(product.shape[1] // LANES):
            value = product[:, b * LANES : (b + 1) * LANES] * scale
            total = total + jnp.sum((value * value).reshape(rows // TILE_S, TILE_S, LANES), axis=0)
            if b < groups:
                send_main[pl.ds(first, half), b, p, :, :] = value.reshape(half, span, LANES)
            else:
                rest_rows[pl.ds(first * span * pair_rows + p, rows, stride=pair_rows), :] = value
        squares[p] = total

        @pl.when(step == 0)
        def _():
            pl.semaphore_wait(barrier, n - 1)

        for early in range(EARLY):
            for h in range(2):
                @pl.when(step == early * 2 + h)
                def _():
                    send(early, h * half, (h + 1) * half)

        return carry

    lax.fori_loop(0, 2 * pair_rows, compute, 0)

    lane = lax.broadcasted_iota(jnp.int32, (pair_rows, LANES), 1)

    def pack(c, carry):
        packed = [jnp.zeros((pair_rows, LANES), jnp.float32)] * (span * rest // LANES)
        for s in range(span):
            at, offset = divmod(s * rest, LANES)
            value = rest_rows[pl.ds(pl.multiple_of((c * span + s) * pair_rows, pair_rows), pair_rows), :]
            if offset:
                value = pltpu.roll(value, offset, axis=1)
            if offset + rest > LANES:
                packed[at] = jnp.where(lane >= offset, value, packed[at])
                packed[at + 1] = jnp.where(lane < offset, value, packed[at + 1])
            else:
                packed[at] = jnp.where(lane >= offset, value, packed[at])
        for b, value in enumerate(packed):
            send_rest[c, :, b * LANES : (b + 1) * LANES] = value
        return carry

    lax.fori_loop(0, n, pack, 0)
    for p in range(pair_rows):
        sq_send[p : p + 1, :] = jnp.sum(squares[p], axis=0, keepdims=True)

    def sq_copy(src, dst, j):
        return pltpu.make_async_remote_copy(
            src_ref=sq_send, dst_ref=sq_recv.at[src],
            send_sem=sq_sems.at[j], recv_sem=sq_recv_sems.at[src],
            device_id={"wide": dst}, device_id_type=MESH,
        )

    def send_squares(j, carry):
        sq_copy(me, lax.rem(me + j, n), j).start()
        return carry

    for i in range(EARLY, len(sets)):
        send(i, 0, n)
        if i == EARLY:
            lax.fori_loop(1, n, send_squares, 0)
    sq_recv[me] = sq_send[...]
    recv_main[:, pl.ds(my_pair, pair_rows), :span, :] = send_main[own]
    recv_rest[pl.ds(my_pair, pair_rows), :] = send_rest[own]

    lines = recv_main.reshape(groups * pairs * stride, LANES)

    def wait_set(i):
        def one(j, carry):
            arrival(i, lax.rem(me + j, n)).wait_recv()
            return carry

        lax.fori_loop(1, n, one, 0)

    for i, (kind, at) in enumerate(sets):
        wait_set(i)
        if kind == "rest":
            for b in range(at * wide * rest // LANES, (at + 1) * wide * rest // LANES):
                for q in range(pairs // LANES):
                    rest_turned[b * LANES : (b + 1) * LANES, q * LANES : (q + 1) * LANES] = (
                        recv_rest[q * LANES : (q + 1) * LANES, b * LANES : (b + 1) * LANES].T
                    )
        elif kind == "main":
            def assemble(k, carry):
                s = at * TILE_S + k
                for b in range(groups):
                    for q in range(pairs // LANES):
                        first = (b * pairs + q * LANES) * stride + s
                        out_ref[s, b * LANES : (b + 1) * LANES, q * LANES : (q + 1) * LANES] = (
                            lines[pl.ds(first, LANES, stride=stride), :].T
                        )
                out_ref[s, full:, :] = rest_turned[pl.ds(pl.multiple_of(s * rest, 8), rest), :]
                return carry

            lax.fori_loop(0, TILE_S, assemble, 0)

    def finish(j, carry):
        src = lax.rem(me + j, n)
        sq_copy(src, src, j).wait_recv()
        sq_copy(me, src, j).wait_send()
        return carry

    lax.fori_loop(1, n, finish, 0)
    for i in range(len(sets)):
        def sent(c, carry):
            remote(i, c, place(c)).wait_send()
            return carry

        lax.fori_loop(0, own, sent, 0)
        lax.fori_loop(own + 1, n, sent, 0)


def finish_kernel(count, main_ref, sq_ref, out_ref, rms_ref, sems):
    parts = sems.shape[0]
    size = main_ref.shape[0] // parts
    copies = [
        pltpu.make_async_copy(main_ref.at[pl.ds(i * size, size)], out_ref.at[pl.ds(i * size, size)], sems.at[i])
        for i in range(parts)
    ]
    for copy in copies:
        copy.start()
    totals = jnp.sum(sq_ref[...].T, axis=0, keepdims=True)
    rms_ref[...] = jnp.sqrt(totals / count + 1e-06)
    for copy in copies:
        copy.wait()


def shards(n, half_integrals, pair_list, occupied_energy, virtual_orbitals, tile_order):
    pair_rows, columns, basis = half_integrals.shape
    virtuals = virtual_orbitals.shape[1]
    pairs = n * pair_rows
    span = columns // n
    deep = round_up(basis, LANES)
    broad = round_up(virtuals, LANES)
    full = virtuals // LANES * LANES
    rest = virtuals - full
    groups = full // LANES
    count = len(schedule(span, rest)[1])
    flops = 6 * pair_rows * columns * basis * virtuals
    vmem = pl.BlockSpec(memory_space=pltpu.VMEM)
    anywhere = pl.BlockSpec(memory_space=pl.ANY)

    def hbm(value):
        return pltpu.with_memory_space_constraint(value, pltpu.HBM)

    main, sq_recv = pl.pallas_call(
        functools.partial(exchange_kernel, n, rest),
        out_shape=(
            pltpu.VMEM((span, virtuals, pairs), jnp.float32),
            pltpu.VMEM((n, pair_rows, LANES), jnp.float32),
        ),
        in_specs=[anywhere] * 5,
        out_specs=(vmem, vmem),
        scratch_shapes=[
            pltpu.SMEM(tile_order.shape, jnp.int32),
            pltpu.VMEM((2, pairs), jnp.int32),
            pltpu.VMEM((1, occupied_energy.shape[0]), jnp.float32),
            pltpu.VMEM((pairs, LANES), jnp.float32),
            pltpu.VMEM((basis, virtuals), jnp.float32),
            pltpu.VMEM((pair_rows, basis, columns), jnp.float32),
            pltpu.VMEM((columns, deep), jnp.float32),
            pltpu.VMEM((columns // 2, deep), jnp.bfloat16),
            pltpu.VMEM((columns // 2, deep), jnp.bfloat16),
            pltpu.VMEM((deep, broad), jnp.bfloat16),
            pltpu.VMEM((deep, broad), jnp.bfloat16),
            pltpu.VMEM((pair_rows, LANES), jnp.float32),
            pltpu.VMEM((pair_rows, TILE_S, LANES), jnp.float32),
            pltpu.VMEM((n, groups, pair_rows, span, LANES), jnp.float32),
            pltpu.VMEM((columns * pair_rows, LANES), jnp.float32),
            pltpu.VMEM((n, pair_rows, span * rest), jnp.float32),
            pltpu.VMEM((pair_rows, LANES), jnp.float32),
            pltpu.VMEM((groups, pairs, span + TILE_S, LANES), jnp.float32),
            pltpu.VMEM((pairs, span * rest), jnp.float32),
            pltpu.VMEM((span * rest, pairs), jnp.float32),
            pltpu.SemaphoreType.DMA((3,)),
            pltpu.SemaphoreType.DMA((1,)),
            pltpu.SemaphoreType.DMA((pair_rows,)),
            pltpu.SemaphoreType.DMA((count, n)),
            pltpu.SemaphoreType.DMA((count, n)),
            pltpu.SemaphoreType.DMA((n,)),
            pltpu.SemaphoreType.DMA((n,)),
        ],
        compiler_params=pltpu.CompilerParams(
            collective_id=0, has_side_effects=True, vmem_limit_bytes=52 * 1024 * 1024
        ),
        cost_estimate=pl.CostEstimate(flops=flops, bytes_accessed=4 * half_integrals.size, transcendentals=0),
        name="exchange",
    )(
        hbm(tile_order), hbm(pair_list.T), hbm(occupied_energy.reshape(1, -1)),
        hbm(jnp.swapaxes(half_integrals, 1, 2)), hbm(virtual_orbitals),
    )
    out, rms = pl.pallas_call(
        functools.partial(finish_kernel, columns * virtuals),
        out_shape=(
            jax.ShapeDtypeStruct((span, virtuals, pairs), jnp.float32),
            jax.ShapeDtypeStruct((1, pairs), jnp.float32),
        ),
        in_specs=[vmem, vmem],
        out_specs=(pl.BlockSpec(memory_space=pltpu.HBM), vmem),
        scratch_shapes=[pltpu.SemaphoreType.DMA((8,))],
        compiler_params=pltpu.CompilerParams(vmem_limit_bytes=2 * 1024 * 1024),
        name="finish",
    )(main, sq_recv.reshape(pairs, LANES))
    return (jnp.transpose(out, (2, 0, 1)), rms.reshape(-1))


def solution(mesh):
    in_specs = (
        P(("groups", "wide"), None, None),
        P("groups", None),
        P("groups"),
        P("groups", None),
        P(),
    )
    out_specs = (P("groups", "wide", None), P("groups"))
    return jax.shard_map(
        functools.partial(shards, mesh.shape["wide"]),
        mesh=mesh, in_specs=in_specs, out_specs=out_specs, check_vma=False,
    )
```

time: 243 us -> 233 us (0.959)
  Pallas kernels: 237 us -> 232 us
  local copies, waits for them, and re-layouts: 3.58 us -> 0 us
    pallas_call x3 -> x2, Pallas kernels: 237 us -> 232 us  [the longest x1 228 us: shards(): pl.pallas_call(functools.partial(exchange_kernel, n, rest), out_shape=(pl...]
    unnamed x8 -> x0, local copies, waits for them, and re-layouts: 3.58 us -> none
where the time goes in v2:
time: 233 us
  Pallas kernels  232 us (100%)
    pallas_call x1, Pallas kernels, shards(): pl.pallas_call(functools.partial(exchange_kernel, n, rest), out_shape=(pl...  228 us

profile of v2, /device:TPU:9, one launch (start us, length us, event | category | flops | bytes accessed | tf_op | source)
XLA Modules:
  0.0 233.1 jit_solution(18412538947857905023)
XLA Ops:
  0.6 228.1 %exchange.1 = (f32[32,600,128]{2,1,0:T(8,128)S(1)}, f32[16,8,128]{2,1,0:T(8,128)S(1)}) custom-call(s32[64]{0:T(128)} %order_hbm.1, s32[2,128]{1,0:T(2,128)} %bitcast.9, f32[1,200]{1,0:T(1,128)} %bitcast.10, f32[8,800,512]{2,1,0:T(8,128)} %bitcast.7, f32[800,600]{1,0:T(8,128)} %w_hbm.1), custom_call_target="tpu_custom_call" | custom-call | flops 11796480000 | bytes 13107200 | tf_op jit(solution)/shard_map/exchange/pallas_call | solution.py:332
  228.8 4.3 %finish.1 = (f32[32,600,128]{2,1,0:T(8,128)}, f32[1,128]{1,0:T(1,128)}) custom-call(f32[32,600,128]{2,1,0:T(8,128)S(1)} %get-tuple-element.6.main_ref, f32[128,128]{1,0:T(8,128)S(1)} %bitcast.6), custom_call_target="tpu_custom_call" | custom-call | tf_op jit(solution)/shard_map/finish/pallas_call | solution.py:378

commit v3 on v2

--- a/solution.py
+++ b/solution.py
@@ -11,6 +11,8 @@
 TILE_S = 8
 LANES = 128
 EARLY = 2
+PARTS = 4
+AHEAD = 2
 MESH = pl.DeviceIdType.MESH
 
 
@@ -34,21 +36,23 @@
 
 
 def exchange_kernel(
-    n, rest, order_hbm, pair_hbm, energy_hbm, x_hbm, w_hbm, out_ref, sq_recv,
+    n, rest, order_hbm, pair_hbm, energy_hbm, x_hbm, w_hbm, out_ref, recv_main, rest_turned, sq_recv,
     order_ref, pair_ref, energy_ref, index_buf, w_buf, x_buf, turned, x_high, x_low, w_high, w_low, scales, squares,
-    send_main, rest_rows, send_rest, sq_send, recv_main, recv_rest, rest_turned,
+    send_main, rest_rows, send_rest, sq_send, recv_rest,
     small_sems, w_sem, x_sems, send_sems, recv_sems, sq_sems, sq_recv_sems,
 ):
     me = lax.axis_index("wide")
     pair_rows, basis, columns = x_hbm.shape
     virtuals = w_hbm.shape[1]
-    span, _, pairs = out_ref.shape
+    pairs = recv_main.shape[1]
+    span = columns // n
     full = virtuals - rest
     deep = turned.shape[1]
     groups = full // LANES
     plane = n // 4
     half = n // 2
-    rows = half * span
+    owners = n // PARTS
+    rows = owners * span
     own = 3 * plane
     owner_tiles = span // TILE_S
     stride = recv_main.shape[2]
@@ -72,12 +76,10 @@
     def fetch(p):
         return pltpu.make_async_copy(x_hbm.at[p], x_buf.at[p], x_sems.at[p])
 
+    fetch(0).start()
     weights_copy.start()
-    fetch(0).start()
     for copy in small:
         copy.start()
-    for p in range(1, pair_rows):
-        fetch(p).start()
     lax.fori_loop(1, n, greet, 0)
 
     sign = 1 - 2 * (me // half)
@@ -104,6 +106,8 @@
         energy = energy + jnp.sum(jnp.where(hit, energy_ref[...], 0.0), axis=1, keepdims=True)
     scales[...] = jnp.broadcast_to(jnp.exp(0.3 * energy), scales.shape)
     weights_copy.wait()
+    for p in range(1, AHEAD):
+        fetch(p).start()
     high, low = split(w_buf[...])
     w_high[:basis, :virtuals] = high
     w_low[:basis, :virtuals] = low
@@ -152,12 +156,17 @@
         lax.fori_loop(max(first, own + 1), last, one, 0)
 
     def compute(step, carry):
-        p = step // 2
-        part = lax.rem(step, 2)
+        p = step // PARTS
+        part = lax.rem(step, PARTS)
 
         @pl.when(part == 0)
         def _():
             fetch(p).wait()
+
+            @pl.when(p + AHEAD < pair_rows)
+            def _():
+                fetch(p + AHEAD).start()
+
             for k in range(deep // LANES):
                 size = min(LANES, basis - k * LANES)
                 for b in range(columns // LANES):
@@ -170,7 +179,7 @@
             pieces = []
             for v in range(2):
                 at = u * 2 + v
-                slot = place(part * half + at // owner_tiles) * owner_tiles + lax.rem(at, owner_tiles)
+                slot = place(part * owners + at // owner_tiles) * owner_tiles + lax.rem(at, owner_tiles)
                 pieces.append(turned[pl.ds(order_ref[slot] * TILE_S, TILE_S), :])
             high, low = split(jnp.concatenate(pieces, axis=0))
             block = pl.ds(pl.multiple_of(u * 2 * TILE_S, 2 * TILE_S), 2 * TILE_S)
@@ -178,18 +187,18 @@
             x_low[block, :] = low
             return carry
 
-        lax.fori_loop(0, rows // TILE_S // 2, gather, 0, unroll=2)
+        lax.fori_loop(0, rows // TILE_S // 2, gather, 0, unroll=8)
         dot = functools.partial(jnp.dot, preferred_element_type=jnp.float32)
         small = dot(x_low[...], w_high[...]) + dot(x_high[...], w_low[...])
         product = dot(x_high[...], w_high[...]) + small
         scale = scales[pl.ds(p, 1), :]
         total = squares[p]
-        first = part * half
+        first = part * owners
         for b in range(product.shape[1] // LANES):
             value = product[:, b * LANES : (b + 1) * LANES] * scale
             total = total + jnp.sum((value * value).reshape(rows // TILE_S, TILE_S, LANES), axis=0)
             if b < groups:
-                send_main[pl.ds(first, half), b, p, :, :] = value.reshape(half, span, LANES)
+                send_main[pl.ds(first, owners), b, p, :, :] = value.reshape(owners, span, LANES)
             else:
                 rest_rows[pl.ds(first * span * pair_rows + p, rows, stride=pair_rows), :] = value
         squares[p] = total
@@ -199,14 +208,14 @@
             pl.semaphore_wait(barrier, n - 1)
 
         for early in range(EARLY):
-            for h in range(2):
-                @pl.when(step == early * 2 + h)
+            for h in range(PARTS):
+                @pl.when(step == early * PARTS + h)
                 def _():
-                    send(early, h * half, (h + 1) * half)
+                    send(early, h * owners, (h + 1) * owners)
 
         return carry
 
-    lax.fori_loop(0, 2 * pair_rows, compute, 0)
+    lax.fori_loop(0, PARTS * pair_rows, compute, 0)
 
     lane = lax.broadcasted_iota(jnp.int32, (pair_rows, LANES), 1)
 
@@ -249,8 +258,6 @@
     recv_main[:, pl.ds(my_pair, pair_rows), :span, :] = send_main[own]
     recv_rest[pl.ds(my_pair, pair_rows), :] = send_rest[own]
 
-    lines = recv_main.reshape(groups * pairs * stride, LANES)
-
     def wait_set(i):
         def one(j, carry):
             arrival(i, lax.rem(me + j, n)).wait_recv()
@@ -258,7 +265,26 @@
 
         lax.fori_loop(1, n, one, 0)
 
+    def sent_set(i):
+        def one(c, carry):
+            remote(i, c, place(c)).wait_send()
+            return carry
+
+        lax.fori_loop(0, own, one, 0)
+        lax.fori_loop(own + 1, n, one, 0)
+
+    def finish(j, carry):
+        src = lax.rem(me + j, n)
+        sq_copy(src, src, j).wait_recv()
+        sq_copy(me, src, j).wait_send()
+        return carry
+
+    last = len(sets) - 1
     for i, (kind, at) in enumerate(sets):
+        if i == last:
+            lax.fori_loop(1, n, finish, 0)
+            for k in range(last):
+                sent_set(k)
         wait_set(i)
         if kind == "rest":
             for b in range(at * wide * rest // LANES, (at + 1) * wide * rest // LANES):
@@ -266,47 +292,47 @@
                     rest_turned[b * LANES : (b + 1) * LANES, q * LANES : (q + 1) * LANES] = (
                         recv_rest[q * LANES : (q + 1) * LANES, b * LANES : (b + 1) * LANES].T
                     )
-        elif kind == "main":
-            def assemble(k, carry):
-                s = at * TILE_S + k
-                for b in range(groups):
-                    for q in range(pairs // LANES):
-                        first = (b * pairs + q * LANES) * stride + s
-                        out_ref[s, b * LANES : (b + 1) * LANES, q * LANES : (q + 1) * LANES] = (
-                            lines[pl.ds(first, LANES, stride=stride), :].T
-                        )
-                out_ref[s, full:, :] = rest_turned[pl.ds(pl.multiple_of(s * rest, 8), rest), :]
+        elif kind == "main" and i < last:
+            def row(k, carry):
+                assemble(recv_main, rest_turned, out_ref, at * TILE_S + k, at * TILE_S + k)
                 return carry
 
-            lax.fori_loop(0, TILE_S, assemble, 0)
-
-    def finish(j, carry):
-        src = lax.rem(me + j, n)
-        sq_copy(src, src, j).wait_recv()
-        sq_copy(me, src, j).wait_send()
-        return carry
-
-    lax.fori_loop(1, n, finish, 0)
-    for i in range(len(sets)):
-        def sent(c, carry):
-            remote(i, c, place(c)).wait_send()
-            return carry
-
-        lax.fori_loop(0, own, sent, 0)
-        lax.fori_loop(own + 1, n, sent, 0)
-
-
-def finish_kernel(count, main_ref, sq_ref, out_ref, rms_ref, sems):
-    parts = sems.shape[0]
-    size = main_ref.shape[0] // parts
+            lax.fori_loop(0, TILE_S, row, 0)
+    sent_set(last)
+
+
+def assemble(recv_main, rest_turned, out_ref, s, to):
+    groups, pairs, stride, _ = recv_main.shape
+    full = groups * LANES
+    rest = out_ref.shape[1] - full
+    lines = recv_main.reshape(groups * pairs * stride, LANES)
+    for b in range(groups):
+        for q in range(pairs // LANES):
+            first = (b * pairs + q * LANES) * stride + s
+            out_ref[to, b * LANES : (b + 1) * LANES, q * LANES : (q + 1) * LANES] = (
+                lines[pl.ds(first, LANES, stride=stride), :].T
+            )
+    out_ref[to, full:, :] = rest_turned[pl.ds(pl.multiple_of(s * rest, 8), rest), :]
+
+
+def finish_kernel(count, main_ref, recv_main, rest_turned, sq_ref, out_ref, rms_ref, tail, rms, sems, tail_sems):
+    done = main_ref.shape[0]
     copies = [
-        pltpu.make_async_copy(main_ref.at[pl.ds(i * size, size)], out_ref.at[pl.ds(i * size, size)], sems.at[i])
-        for i in range(parts)
+        pltpu.make_async_copy(main_ref.at[pl.ds(k, TILE_S)], out_ref.at[pl.ds(k, TILE_S)], sems.at[k // TILE_S])
+        for k in range(0, done, TILE_S)
     ]
     for copy in copies:
         copy.start()
     totals = jnp.sum(sq_ref[...].T, axis=0, keepdims=True)
-    rms_ref[...] = jnp.sqrt(totals / count + 1e-06)
+    rms[...] = jnp.sqrt(totals / count + 1e-06)
+    rms_copy = pltpu.make_async_copy(rms, rms_ref, tail_sems.at[tail.shape[0]])
+    rms_copy.start()
+    copies.append(rms_copy)
+    for k in range(tail.shape[0]):
+        assemble(recv_main, rest_turned, tail, done + k, k)
+        copy = pltpu.make_async_copy(tail.at[k], out_ref.at[done + k], tail_sems.at[k])
+        copy.start()
+        copies.append(copy)
     for copy in copies:
         copy.wait()
 
@@ -329,14 +355,16 @@
     def hbm(value):
         return pltpu.with_memory_space_constraint(value, pltpu.HBM)
 
-    main, sq_recv = pl.pallas_call(
+    main, recv_main, rest_turned, sq_recv = pl.pallas_call(
         functools.partial(exchange_kernel, n, rest),
         out_shape=(
-            pltpu.VMEM((span, virtuals, pairs), jnp.float32),
+            pltpu.VMEM((span - TILE_S, virtuals, pairs), jnp.float32),
+            pltpu.VMEM((groups, pairs, span + TILE_S, LANES), jnp.float32),
+            pltpu.VMEM((span * rest, pairs), jnp.float32),
             pltpu.VMEM((n, pair_rows, LANES), jnp.float32),
         ),
         in_specs=[anywhere] * 5,
-        out_specs=(vmem, vmem),
+        out_specs=(vmem,) * 4,
         scratch_shapes=[
             pltpu.SMEM(tile_order.shape, jnp.int32),
             pltpu.VMEM((2, pairs), jnp.int32),
@@ -345,8 +373,8 @@
             pltpu.VMEM((basis, virtuals), jnp.float32),
             pltpu.VMEM((pair_rows, basis, columns), jnp.float32),
             pltpu.VMEM((columns, deep), jnp.float32),
-            pltpu.VMEM((columns // 2, deep), jnp.bfloat16),
-            pltpu.VMEM((columns // 2, deep), jnp.bfloat16),
+            pltpu.VMEM((columns // PARTS, deep), jnp.bfloat16),
+            pltpu.VMEM((columns // PARTS, deep), jnp.bfloat16),
             pltpu.VMEM((deep, broad), jnp.bfloat16),
             pltpu.VMEM((deep, broad), jnp.bfloat16),
             pltpu.VMEM((pair_rows, LANES), jnp.float32),
@@ -355,9 +383,7 @@
             pltpu.VMEM((columns * pair_rows, LANES), jnp.float32),
             pltpu.VMEM((n, pair_rows, span * rest), jnp.float32),
             pltpu.VMEM((pair_rows, LANES), jnp.float32),
-            pltpu.VMEM((groups, pairs, span + TILE_S, LANES), jnp.float32),
             pltpu.VMEM((pairs, span * rest), jnp.float32),
-            pltpu.VMEM((span * rest, pairs), jnp.float32),
             pltpu.SemaphoreType.DMA((3,)),
             pltpu.SemaphoreType.DMA((1,)),
             pltpu.SemaphoreType.DMA((pair_rows,)),
@@ -367,7 +393,7 @@
             pltpu.SemaphoreType.DMA((n,)),
         ],
         compiler_params=pltpu.CompilerParams(
-            collective_id=0, has_side_effects=True, vmem_limit_bytes=52 * 1024 * 1024
+            collective_id=0, has_side_effects=True, vmem_limit_bytes=42 * 1024 * 1024
         ),
         cost_estimate=pl.CostEstimate(flops=flops, bytes_accessed=4 * half_integrals.size, transcendentals=0),
         name="exchange",
@@ -381,12 +407,17 @@
             jax.ShapeDtypeStruct((span, virtuals, pairs), jnp.float32),
             jax.ShapeDtypeStruct((1, pairs), jnp.float32),
         ),
-        in_specs=[vmem, vmem],
-        out_specs=(pl.BlockSpec(memory_space=pltpu.HBM), vmem),
-        scratch_shapes=[pltpu.SemaphoreType.DMA((8,))],
-        compiler_params=pltpu.CompilerParams(vmem_limit_bytes=2 * 1024 * 1024),
+        in_specs=[vmem] * 4,
+        out_specs=(pl.BlockSpec(memory_space=pltpu.HBM),) * 2,
+        scratch_shapes=[
+            pltpu.VMEM((TILE_S, virtuals, pairs), jnp.float32),
+            pltpu.VMEM((1, pairs), jnp.float32),
+            pltpu.SemaphoreType.DMA((span // TILE_S - 1,)),
+            pltpu.SemaphoreType.DMA((TILE_S + 1,)),
+        ],
+        compiler_params=pltpu.CompilerParams(vmem_limit_bytes=8 * 1024 * 1024),
         name="finish",
-    )(main, sq_recv.reshape(pairs, LANES))
+    )(main, recv_main, rest_turned, sq_recv.reshape(pairs, LANES))
     return (jnp.transpose(out, (2, 0, 1)), rms.reshape(-1))
 
 

time: 233 us -> 227 us (0.974)
  Pallas kernels: 232 us -> 226 us
    pallas_call x1, Pallas kernels: 228 us -> 222 us  [shards(): pl.pallas_call(functools.partial(exchange_kernel, n, rest), out_shape=(pl...]
where the time goes in v3:
time: 227 us
  Pallas kernels  226 us (100%)
    pallas_call x1, Pallas kernels, shards(): pl.pallas_call(functools.partial(exchange_kernel, n, rest), out_shape=(pl...  222 us

profile of v3, /device:TPU:9, one launch (start us, length us, event | category | flops | bytes accessed | tf_op | source)
XLA Modules:
  0.0 226.6 jit_solution(8306998660052588032)
XLA Ops:
  0.6 222.1 %exchange.1 = (f32[24,600,128]{2,1,0:T(8,128)S(1)}, f32[4,128,40,128]{3,2,1,0:T(8,128)S(1)}, f32[2816,128]{1,0:T(8,128)S(1)}, f32[16,8,128]{2,1,0:T(8,128)S(1)}) custom-call(s32[64]{0:T(128)} %order_hbm.1, s32[2,128]{1,0:T(2,128)} %bitcast.9, f32[1,200]{1,0:T(1,128)} %bitcast.10, f32[8,800,512]{2,1,0:T(8,128)} %bitcast.7, f32[800,600]{1,0:T(8,128)} %w_hbm.1), custom_call_target="tpu_custom_call" | custom-call | flops 11796480000 | bytes 13107200 | tf_op jit(solution)/shard_map/exchange/pallas_call | solution.py:358
  222.8 3.9 %finish.1 = (f32[32,600,128]{2,1,0:T(8,128)}, f32[1,128]{1,0:T(1,128)}) custom-call(f32[24,600,128]{2,1,0:T(8,128)S(1)} %get-tuple-element.8.main_ref, f32[4,128,40,128]{3,2,1,0:T(8,128)S(1)} %get-tuple-element.9.recv_main, f32[2816,128]{1,0:T(8,128)S(1)} %get-tuple-element.10.rest_turned, f32[128,128]{1,0:T(8,128)S(1)} %bitcast.6), custom_call_target="tpu_custom_call" | custom-call | tf_op jit(solution)/shard_map/finish/pallas_call | solution.py:404

commit v4 on v3

--- a/solution.py
+++ b/solution.py
@@ -39,7 +39,7 @@
     n, rest, order_hbm, pair_hbm, energy_hbm, x_hbm, w_hbm, out_ref, recv_main, rest_turned, sq_recv,
     order_ref, pair_ref, energy_ref, index_buf, w_buf, x_buf, turned, x_high, x_low, w_high, w_low, scales, squares,
     send_main, rest_rows, send_rest, sq_send, recv_rest,
-    small_sems, w_sem, x_sems, send_sems, recv_sems, sq_sems, sq_recv_sems,
+    small_sems, w_sem, x_sems, send_sems, recv_sems, sq_sems,
 ):
     me = lax.axis_index("wide")
     pair_rows, basis, columns = x_hbm.shape
@@ -74,7 +74,7 @@
     weights_copy = pltpu.make_async_copy(w_hbm, w_buf, w_sem.at[0])
 
     def fetch(p):
-        return pltpu.make_async_copy(x_hbm.at[p], x_buf.at[p], x_sems.at[p])
+        return pltpu.make_async_copy(x_hbm.at[p], x_buf.at[p], x_sems.at[lax.rem(p, AHEAD)])
 
     fetch(0).start()
     weights_copy.start()
@@ -125,27 +125,24 @@
             src = send_rest.at[c, :, lanes]
             dst = recv_rest.at[pl.ds(my_pair, pair_rows), lanes]
         return pltpu.make_async_remote_copy(
-            src_ref=src, dst_ref=dst, send_sem=send_sems.at[i, c], recv_sem=recv_sems.at[i, me],
+            src_ref=src, dst_ref=dst, send_sem=send_sems.at[i], recv_sem=recv_sems.at[i],
             device_id={"wide": owner}, device_id_type=MESH,
         )
 
-    def arrival(i, src):
+    def wait_all(i, received):
         kind, at = sets[i]
-        first = pl.multiple_of(src * pair_rows, pair_rows)
         if kind == "pair":
-            local = send_main.at[0, :, at, :, :]
-            dst = recv_main.at[:, first + at, pl.ds(0, span), :]
+            src = send_main.at[pl.ds(0, n - 1), :, at, :, :]
+            dst = recv_main.at[:, pl.ds(0, n - 1), pl.ds(0, span), :]
         elif kind == "main":
-            local = send_main.at[0, :, pl.ds(EARLY, late), pl.ds(at * TILE_S, TILE_S), :]
-            dst = recv_main.at[:, pl.ds(first + EARLY, late), pl.ds(at * TILE_S, TILE_S), :]
+            src = send_main.at[pl.ds(0, n - 1), :, pl.ds(EARLY, late), pl.ds(at * TILE_S, TILE_S), :]
+            dst = recv_main.at[:, pl.ds(0, late * (n - 1)), pl.ds(at * TILE_S, TILE_S), :]
         else:
             lanes = pl.ds(at * wide * rest, wide * rest)
-            local = send_rest.at[0, :, lanes]
-            dst = recv_rest.at[pl.ds(first, pair_rows), lanes]
-        return pltpu.make_async_remote_copy(
-            src_ref=local, dst_ref=dst, send_sem=send_sems.at[i, 0], recv_sem=recv_sems.at[i, src],
-            device_id={"wide": src}, device_id_type=MESH,
-        )
+            src = send_rest.at[pl.ds(0, n - 1), :, lanes]
+            dst = recv_rest.at[pl.ds(0, pair_rows * (n - 1)), lanes]
+        ref, sem = (dst, recv_sems.at[i]) if received else (src, send_sems.at[i])
+        pltpu.make_async_copy(ref, ref, sem).wait()
 
     def send(i, first, last):
         def one(c, carry):
@@ -236,18 +233,22 @@
         return carry
 
     lax.fori_loop(0, n, pack, 0)
+    pair_lane = lax.broadcasted_iota(jnp.int32, (1, pairs), 1) - my_pair
+    total = jnp.zeros((1, pairs), jnp.float32)
     for p in range(pair_rows):
-        sq_send[p : p + 1, :] = jnp.sum(squares[p], axis=0, keepdims=True)
-
-    def sq_copy(src, dst, j):
+        value = jnp.sum(jnp.sum(squares[p], axis=0, keepdims=True), axis=1, keepdims=True)
+        total = jnp.where(pair_lane == p, value, total)
+    sq_send[...] = total
+
+    def sq_copy(dst):
         return pltpu.make_async_remote_copy(
-            src_ref=sq_send, dst_ref=sq_recv.at[src],
-            send_sem=sq_sems.at[j], recv_sem=sq_recv_sems.at[src],
+            src_ref=sq_send, dst_ref=sq_recv.at[me],
+            send_sem=sq_sems.at[0], recv_sem=sq_sems.at[1],
             device_id={"wide": dst}, device_id_type=MESH,
         )
 
     def send_squares(j, carry):
-        sq_copy(me, lax.rem(me + j, n), j).start()
+        sq_copy(lax.rem(me + j, n)).start()
         return carry
 
     for i in range(EARLY, len(sets)):
@@ -258,34 +259,15 @@
     recv_main[:, pl.ds(my_pair, pair_rows), :span, :] = send_main[own]
     recv_rest[pl.ds(my_pair, pair_rows), :] = send_rest[own]
 
-    def wait_set(i):
-        def one(j, carry):
-            arrival(i, lax.rem(me + j, n)).wait_recv()
-            return carry
-
-        lax.fori_loop(1, n, one, 0)
-
-    def sent_set(i):
-        def one(c, carry):
-            remote(i, c, place(c)).wait_send()
-            return carry
-
-        lax.fori_loop(0, own, one, 0)
-        lax.fori_loop(own + 1, n, one, 0)
-
-    def finish(j, carry):
-        src = lax.rem(me + j, n)
-        sq_copy(src, src, j).wait_recv()
-        sq_copy(me, src, j).wait_send()
-        return carry
-
     last = len(sets) - 1
     for i, (kind, at) in enumerate(sets):
         if i == last:
-            lax.fori_loop(1, n, finish, 0)
+            others = sq_recv.at[pl.ds(0, n - 1)]
+            pltpu.make_async_copy(others, others, sq_sems.at[0]).wait()
+            pltpu.make_async_copy(others, others, sq_sems.at[1]).wait()
             for k in range(last):
-                sent_set(k)
-        wait_set(i)
+                wait_all(k, False)
+        wait_all(i, True)
         if kind == "rest":
             for b in range(at * wide * rest // LANES, (at + 1) * wide * rest // LANES):
                 for q in range(pairs // LANES):
@@ -298,7 +280,7 @@
                 return carry
 
             lax.fori_loop(0, TILE_S, row, 0)
-    sent_set(last)
+    wait_all(last, False)
 
 
 def assemble(recv_main, rest_turned, out_ref, s, to):
@@ -323,7 +305,7 @@
     ]
     for copy in copies:
         copy.start()
-    totals = jnp.sum(sq_ref[...].T, axis=0, keepdims=True)
+    totals = jnp.sum(sq_ref[...], axis=0)
     rms[...] = jnp.sqrt(totals / count + 1e-06)
     rms_copy = pltpu.make_async_copy(rms, rms_ref, tail_sems.at[tail.shape[0]])
     rms_copy.start()
@@ -361,7 +343,7 @@
             pltpu.VMEM((span - TILE_S, virtuals, pairs), jnp.float32),
             pltpu.VMEM((groups, pairs, span + TILE_S, LANES), jnp.float32),
             pltpu.VMEM((span * rest, pairs), jnp.float32),
-            pltpu.VMEM((n, pair_rows, LANES), jnp.float32),
+            pltpu.VMEM((n, 1, pairs), jnp.float32),
         ),
         in_specs=[anywhere] * 5,
         out_specs=(vmem,) * 4,
@@ -382,15 +364,14 @@
             pltpu.VMEM((n, groups, pair_rows, span, LANES), jnp.float32),
             pltpu.VMEM((columns * pair_rows, LANES), jnp.float32),
             pltpu.VMEM((n, pair_rows, span * rest), jnp.float32),
-            pltpu.VMEM((pair_rows, LANES), jnp.float32),
+            pltpu.VMEM((1, pairs), jnp.float32),
             pltpu.VMEM((pairs, span * rest), jnp.float32),
             pltpu.SemaphoreType.DMA((3,)),
             pltpu.SemaphoreType.DMA((1,)),
-            pltpu.SemaphoreType.DMA((pair_rows,)),
-            pltpu.SemaphoreType.DMA((count, n)),
-            pltpu.SemaphoreType.DMA((count, n)),
-            pltpu.SemaphoreType.DMA((n,)),
-            pltpu.SemaphoreType.DMA((n,)),
+            pltpu.SemaphoreType.DMA((AHEAD,)),
+            pltpu.SemaphoreType.DMA((count,)),
+            pltpu.SemaphoreType.DMA((count,)),
+            pltpu.SemaphoreType.DMA((2,)),
         ],
         compiler_params=pltpu.CompilerParams(
             collective_id=0, has_side_effects=True, vmem_limit_bytes=42 * 1024 * 1024
@@ -417,7 +398,7 @@
         ],
         compiler_params=pltpu.CompilerParams(vmem_limit_bytes=8 * 1024 * 1024),
         name="finish",
-    )(main, recv_main, rest_turned, sq_recv.reshape(pairs, LANES))
+    )(main, recv_main, rest_turned, sq_recv)
     return (jnp.transpose(out, (2, 0, 1)), rms.reshape(-1))
 
 

time: 227 us -> 223 us (0.982)
  Pallas kernels: 226 us -> 222 us
    pallas_call x1, Pallas kernels: 222 us -> 218 us  [shards(): pl.pallas_call(functools.partial(exchange_kernel, n, rest), out_shape=(pl...]
where the time goes in v4:
time: 223 us
  Pallas kernels  222 us (100%)
    pallas_call x1, Pallas kernels, shards(): pl.pallas_call(functools.partial(exchange_kernel, n, rest), out_shape=(pl...  218 us

profile of v4, /device:TPU:9, one launch (start us, length us, event | category | flops | bytes accessed | tf_op | source)
XLA Modules:
  0.0 222.8 jit_solution(6862599498972121352)
XLA Ops:
  0.6 218.3 %exchange.1 = (f32[24,600,128]{2,1,0:T(8,128)S(1)}, f32[4,128,40,128]{3,2,1,0:T(8,128)S(1)}, f32[2816,128]{1,0:T(8,128)S(1)}, f32[16,1,128]{2,1,0:T(1,128)S(1)}) custom-call(s32[64]{0:T(128)} %order_hbm.1, s32[2,128]{1,0:T(2,128)} %bitcast.7, f32[1,200]{1,0:T(1,128)} %bitcast.8, f32[8,800,512]{2,1,0:T(8,128)} %bitcast.5, f32[800,600]{1,0:T(8,128)} %w_hbm.1), custom_call_target="tpu_custom_call" | custom-call | flops 11796480000 | bytes 13107200 | tf_op jit(solution)/shard_map/exchange/pallas_call | solution.py:340
  219.0 3.8 %finish.1 = (f32[32,600,128]{2,1,0:T(8,128)}, f32[1,128]{1,0:T(1,128)}) custom-call(f32[24,600,128]{2,1,0:T(8,128)S(1)} %get-tuple-element.8.main_ref, f32[4,128,40,128]{3,2,1,0:T(8,128)S(1)} %get-tuple-element.9.recv_main, f32[2816,128]{1,0:T(8,128)S(1)} %get-tuple-element.10.rest_turned, f32[16,1,128]{2,1,0:T(1,128)S(1)} %get-tuple-element.11.sq_ref), custom_call_target="tpu_custom_call" | custom-call | tf_op jit(solution)/shard_map/finish/pallas_call | solution.py:385

commit v5 on v4

--- a/solution.py
+++ b/solution.py
@@ -12,7 +12,6 @@
 LANES = 128
 EARLY = 2
 PARTS = 4
-AHEAD = 2
 MESH = pl.DeviceIdType.MESH
 
 
@@ -39,7 +38,7 @@
     n, rest, order_hbm, pair_hbm, energy_hbm, x_hbm, w_hbm, out_ref, recv_main, rest_turned, sq_recv,
     order_ref, pair_ref, energy_ref, index_buf, w_buf, x_buf, turned, x_high, x_low, w_high, w_low, scales, squares,
     send_main, rest_rows, send_rest, sq_send, recv_rest,
-    small_sems, w_sem, x_sems, send_sems, recv_sems, sq_sems,
+    small_sems, w_sem, x_sem, send_sems, recv_sems, sq_sems,
 ):
     me = lax.axis_index("wide")
     pair_rows, basis, columns = x_hbm.shape
@@ -74,13 +73,13 @@
     weights_copy = pltpu.make_async_copy(w_hbm, w_buf, w_sem.at[0])
 
     def fetch(p):
-        return pltpu.make_async_copy(x_hbm.at[p], x_buf.at[p], x_sems.at[lax.rem(p, AHEAD)])
-
-    fetch(0).start()
+        return pltpu.make_async_copy(x_hbm.at[p], x_buf.at[p], x_sem.at[0])
+
     weights_copy.start()
     for copy in small:
         copy.start()
-    lax.fori_loop(1, n, greet, 0)
+    fetch(0).start()
+    lax.fori_loop(1, n, greet, 0, unroll=5)
 
     sign = 1 - 2 * (me // half)
     my_plane = me // plane
@@ -106,8 +105,6 @@
         energy = energy + jnp.sum(jnp.where(hit, energy_ref[...], 0.0), axis=1, keepdims=True)
     scales[...] = jnp.broadcast_to(jnp.exp(0.3 * energy), scales.shape)
     weights_copy.wait()
-    for p in range(1, AHEAD):
-        fetch(p).start()
     high, low = split(w_buf[...])
     w_high[:basis, :virtuals] = high
     w_low[:basis, :virtuals] = low
@@ -144,9 +141,10 @@
         ref, sem = (dst, recv_sems.at[i]) if received else (src, send_sems.at[i])
         pltpu.make_async_copy(ref, ref, sem).wait()
 
-    def send(i, first, last):
+    def send(kinds, first, last):
         def one(c, carry):
-            remote(i, c, place(c)).start()
+            for i in kinds:
+                remote(i, c, place(c)).start()
             return carry
 
         lax.fori_loop(first, min(last, own), one, 0)
@@ -160,9 +158,9 @@
         def _():
             fetch(p).wait()
 
-            @pl.when(p + AHEAD < pair_rows)
+            @pl.when(p + 1 < pair_rows)
             def _():
-                fetch(p + AHEAD).start()
+                fetch(p + 1).start()
 
             for k in range(deep // LANES):
                 size = min(LANES, basis - k * LANES)
@@ -208,7 +206,7 @@
             for h in range(PARTS):
                 @pl.when(step == early * PARTS + h)
                 def _():
-                    send(early, h * owners, (h + 1) * owners)
+                    send([early], h * owners, (h + 1) * owners)
 
         return carry
 
@@ -251,15 +249,14 @@
         sq_copy(lax.rem(me + j, n)).start()
         return carry
 
-    for i in range(EARLY, len(sets)):
-        send(i, 0, n)
-        if i == EARLY:
-            lax.fori_loop(1, n, send_squares, 0)
+    last = len(sets) - 1
+    lax.fori_loop(1, n, send_squares, 0)
+    send(range(EARLY, last), 0, n)
+    send([last], 0, n)
     sq_recv[me] = sq_send[...]
     recv_main[:, pl.ds(my_pair, pair_rows), :span, :] = send_main[own]
     recv_rest[pl.ds(my_pair, pair_rows), :] = send_rest[own]
 
-    last = len(sets) - 1
     for i, (kind, at) in enumerate(sets):
         if i == last:
             others = sq_recv.at[pl.ds(0, n - 1)]
@@ -297,26 +294,19 @@
     out_ref[to, full:, :] = rest_turned[pl.ds(pl.multiple_of(s * rest, 8), rest), :]
 
 
-def finish_kernel(count, main_ref, recv_main, rest_turned, sq_ref, out_ref, rms_ref, tail, rms, sems, tail_sems):
+def finish_kernel(count, main_ref, recv_main, rest_turned, sq_ref, out_ref, rms_ref, tail, rms, sems):
     done = main_ref.shape[0]
-    copies = [
-        pltpu.make_async_copy(main_ref.at[pl.ds(k, TILE_S)], out_ref.at[pl.ds(k, TILE_S)], sems.at[k // TILE_S])
-        for k in range(0, done, TILE_S)
-    ]
-    for copy in copies:
-        copy.start()
+    rows = tail.shape[0]
+    pltpu.make_async_copy(main_ref, out_ref.at[pl.ds(0, done)], sems.at[0]).start()
     totals = jnp.sum(sq_ref[...], axis=0)
     rms[...] = jnp.sqrt(totals / count + 1e-06)
-    rms_copy = pltpu.make_async_copy(rms, rms_ref, tail_sems.at[tail.shape[0]])
-    rms_copy.start()
-    copies.append(rms_copy)
-    for k in range(tail.shape[0]):
+    pltpu.make_async_copy(rms, rms_ref, sems.at[2]).start()
+    for k in range(rows):
         assemble(recv_main, rest_turned, tail, done + k, k)
-        copy = pltpu.make_async_copy(tail.at[k], out_ref.at[done + k], tail_sems.at[k])
-        copy.start()
-        copies.append(copy)
-    for copy in copies:
-        copy.wait()
+        pltpu.make_async_copy(tail.at[k], out_ref.at[done + k], sems.at[1]).start()
+    pltpu.make_async_copy(tail, out_ref.at[pl.ds(done, rows)], sems.at[1]).wait()
+    pltpu.make_async_copy(rms, rms_ref, sems.at[2]).wait()
+    pltpu.make_async_copy(main_ref, out_ref.at[pl.ds(0, done)], sems.at[0]).wait()
 
 
 def shards(n, half_integrals, pair_list, occupied_energy, virtual_orbitals, tile_order):
@@ -368,7 +358,7 @@
             pltpu.VMEM((pairs, span * rest), jnp.float32),
             pltpu.SemaphoreType.DMA((3,)),
             pltpu.SemaphoreType.DMA((1,)),
-            pltpu.SemaphoreType.DMA((AHEAD,)),
+            pltpu.SemaphoreType.DMA((1,)),
             pltpu.SemaphoreType.DMA((count,)),
             pltpu.SemaphoreType.DMA((count,)),
             pltpu.SemaphoreType.DMA((2,)),
@@ -393,8 +383,7 @@
         scratch_shapes=[
             pltpu.VMEM((TILE_S, virtuals, pairs), jnp.float32),
             pltpu.VMEM((1, pairs), jnp.float32),
-            pltpu.SemaphoreType.DMA((span // TILE_S - 1,)),
-            pltpu.SemaphoreType.DMA((TILE_S + 1,)),
+            pltpu.SemaphoreType.DMA((3,)),
         ],
         compiler_params=pltpu.CompilerParams(vmem_limit_bytes=8 * 1024 * 1024),
         name="finish",

time: 223 us -> 223 us (level)
  no operation moved by 1% of the time
where the time goes in v5:
time: 223 us; the launch traced here: 222 us
  Pallas kernels  222 us (100%)
    pallas_call x1, Pallas kernels, shards(): pl.pallas_call(functools.partial(exchange_kernel, n, rest), out_shape=(pl...  218 us

profile of v5, /device:TPU:9, one launch (start us, length us, event | category | flops | bytes accessed | tf_op | source)
XLA Modules:
  0.0 222.4 jit_solution(13246696976759770622)
XLA Ops:
  0.6 217.9 %exchange.1 = (f32[24,600,128]{2,1,0:T(8,128)S(1)}, f32[4,128,40,128]{3,2,1,0:T(8,128)S(1)}, f32[2816,128]{1,0:T(8,128)S(1)}, f32[16,1,128]{2,1,0:T(1,128)S(1)}) custom-call(s32[64]{0:T(128)} %order_hbm.1, s32[2,128]{1,0:T(2,128)} %bitcast.7, f32[1,200]{1,0:T(1,128)} %bitcast.8, f32[8,800,512]{2,1,0:T(8,128)} %bitcast.5, f32[800,600]{1,0:T(8,128)} %w_hbm.1), custom_call_target="tpu_custom_call" | custom-call | flops 11796480000 | bytes 13107200 | tf_op jit(solution)/shard_map/exchange/pallas_call | solution.py:330
  218.6 3.8 %finish.1 = (f32[32,600,128]{2,1,0:T(8,128)}, f32[1,128]{1,0:T(1,128)}) custom-call(f32[24,600,128]{2,1,0:T(8,128)S(1)} %get-tuple-element.8.main_ref, f32[4,128,40,128]{3,2,1,0:T(8,128)S(1)} %get-tuple-element.9.recv_main, f32[2816,128]{1,0:T(8,128)S(1)} %get-tuple-element.10.rest_turned, f32[16,1,128]{2,1,0:T(1,128)S(1)} %get-tuple-element.11.sq_ref), custom_call_target="tpu_custom_call" | custom-call | tf_op jit(solution)/shard_map/finish/pallas_call | solution.py:375

commit v6 on v5

--- a/solution.py
+++ b/solution.py
@@ -301,9 +301,14 @@
     totals = jnp.sum(sq_ref[...], axis=0)
     rms[...] = jnp.sqrt(totals / count + 1e-06)
     pltpu.make_async_copy(rms, rms_ref, sems.at[2]).start()
+    def write(k):
+        return pltpu.make_async_copy(tail.at[k], out_ref.at[done + k], sems.at[1])
+
     for k in range(rows):
         assemble(recv_main, rest_turned, tail, done + k, k)
-        pltpu.make_async_copy(tail.at[k], out_ref.at[done + k], sems.at[1]).start()
+        if k:
+            write(k - 1).start()
+    write(rows - 1).start()
     pltpu.make_async_copy(tail, out_ref.at[pl.ds(done, rows)], sems.at[1]).wait()
     pltpu.make_async_copy(rms, rms_ref, sems.at[2]).wait()
     pltpu.make_async_copy(main_ref, out_ref.at[pl.ds(0, done)], sems.at[0]).wait()

time: 223 us -> 223 us (level)
  no operation moved by 1% of the time
where the time goes in v6:
time: 223 us; the launch traced here: 222 us
  Pallas kernels  222 us (100%)
    pallas_call x1, Pallas kernels, shards(): pl.pallas_call(functools.partial(exchange_kernel, n, rest), out_shape=(pl...  218 us

profile of v6, /device:TPU:9, one launch (start us, length us, event | category | flops | bytes accessed | tf_op | source)
XLA Modules:
  0.0 222.4 jit_solution(5026750502691304104)
XLA Ops:
  0.6 217.9 %exchange.1 = (f32[24,600,128]{2,1,0:T(8,128)S(1)}, f32[4,128,40,128]{3,2,1,0:T(8,128)S(1)}, f32[2816,128]{1,0:T(8,128)S(1)}, f32[16,1,128]{2,1,0:T(1,128)S(1)}) custom-call(s32[64]{0:T(128)} %order_hbm.1, s32[2,128]{1,0:T(2,128)} %bitcast.7, f32[1,200]{1,0:T(1,128)} %bitcast.8, f32[8,800,512]{2,1,0:T(8,128)} %bitcast.5, f32[800,600]{1,0:T(8,128)} %w_hbm.1), custom_call_target="tpu_custom_call" | custom-call | flops 11796480000 | bytes 13107200 | tf_op jit(solution)/shard_map/exchange/pallas_call | solution.py:335
  218.6 3.8 %finish.1 = (f32[32,600,128]{2,1,0:T(8,128)}, f32[1,128]{1,0:T(1,128)}) custom-call(f32[24,600,128]{2,1,0:T(8,128)S(1)} %get-tuple-element.8.main_ref, f32[4,128,40,128]{3,2,1,0:T(8,128)S(1)} %get-tuple-element.9.recv_main, f32[2816,128]{1,0:T(8,128)S(1)} %get-tuple-element.10.rest_turned, f32[16,1,128]{2,1,0:T(1,128)S(1)} %get-tuple-element.11.sq_ref), custom_call_target="tpu_custom_call" | custom-call | tf_op jit(solution)/shard_map/finish/pallas_call | solution.py:380

commit v7 on v6

--- a/solution.py
+++ b/solution.py
@@ -10,7 +10,7 @@
 
 TILE_S = 8
 LANES = 128
-EARLY = 2
+EARLY = 3
 PARTS = 4
 MESH = pl.DeviceIdType.MESH
 
@@ -36,7 +36,7 @@
 
 def exchange_kernel(
     n, rest, order_hbm, pair_hbm, energy_hbm, x_hbm, w_hbm, out_ref, recv_main, rest_turned, sq_recv,
-    order_ref, pair_ref, energy_ref, index_buf, w_buf, x_buf, turned, x_high, x_low, w_high, w_low, scales, squares,
+    order_ref, pair_ref, energy_ref, index_buf, w_buf, x_buf, turned, x_split, w_split, scales, squares,
     send_main, rest_rows, send_rest, sq_send, recv_rest,
     small_sems, w_sem, x_sem, send_sems, recv_sems, sq_sems,
 ):
@@ -91,8 +91,7 @@
         return (my_plane + sign * away) * plane + lax.rem(me + c, plane)
 
     squares[...] = jnp.zeros_like(squares)
-    w_high[...] = jnp.zeros_like(w_high)
-    w_low[...] = jnp.zeros_like(w_low)
+    w_split[...] = jnp.zeros_like(w_split)
     for copy in small:
         copy.wait()
     orbitals = energy_ref.shape[1]
@@ -106,8 +105,8 @@
     scales[...] = jnp.broadcast_to(jnp.exp(0.3 * energy), scales.shape)
     weights_copy.wait()
     high, low = split(w_buf[...])
-    w_high[:basis, :virtuals] = high
-    w_low[:basis, :virtuals] = low
+    for k, value in enumerate((high, high, low)):
+        w_split[k * deep : k * deep + basis, :virtuals] = value
 
     def remote(i, c, owner):
         kind, at = sets[i]
@@ -178,14 +177,12 @@
                 pieces.append(turned[pl.ds(order_ref[slot] * TILE_S, TILE_S), :])
             high, low = split(jnp.concatenate(pieces, axis=0))
             block = pl.ds(pl.multiple_of(u * 2 * TILE_S, 2 * TILE_S), 2 * TILE_S)
-            x_high[block, :] = high
-            x_low[block, :] = low
+            for k, value in enumerate((high, low, high)):
+                x_split[block, k * deep : (k + 1) * deep] = value
             return carry
 
         lax.fori_loop(0, rows // TILE_S // 2, gather, 0, unroll=8)
-        dot = functools.partial(jnp.dot, preferred_element_type=jnp.float32)
-        small = dot(x_low[...], w_high[...]) + dot(x_high[...], w_low[...])
-        product = dot(x_high[...], w_high[...]) + small
+        product = jnp.dot(x_split[...], w_split[...], preferred_element_type=jnp.float32)
         scale = scales[pl.ds(p, 1), :]
         total = squares[p]
         first = part * owners
@@ -350,10 +347,8 @@
             pltpu.VMEM((basis, virtuals), jnp.float32),
             pltpu.VMEM((pair_rows, basis, columns), jnp.float32),
             pltpu.VMEM((columns, deep), jnp.float32),
-            pltpu.VMEM((columns // PARTS, deep), jnp.bfloat16),
-            pltpu.VMEM((columns // PARTS, deep), jnp.bfloat16),
-            pltpu.VMEM((deep, broad), jnp.bfloat16),
-            pltpu.VMEM((deep, broad), jnp.bfloat16),
+            pltpu.VMEM((columns // PARTS, 3 * deep), jnp.bfloat16),
+            pltpu.VMEM((3 * deep, broad), jnp.bfloat16),
             pltpu.VMEM((pair_rows, LANES), jnp.float32),
             pltpu.VMEM((pair_rows, TILE_S, LANES), jnp.float32),
             pltpu.VMEM((n, groups, pair_rows, span, LANES), jnp.float32),

time: 223 us -> 222 us (level)
  no operation moved by 1% of the time
where the time goes in v7:
time: 222 us
  Pallas kernels  222 us (100%)
    pallas_call x1, Pallas kernels, shards(): pl.pallas_call(functools.partial(exchange_kernel, n, rest), out_shape=(pl...  218 us

profile of v7, /device:TPU:9, one launch (start us, length us, event | category | flops | bytes accessed | tf_op | source)
XLA Modules:
  0.0 222.3 jit_solution(5224543925873471891)
XLA Ops:
  0.6 217.8 %exchange.1 = (f32[24,600,128]{2,1,0:T(8,128)S(1)}, f32[4,128,40,128]{3,2,1,0:T(8,128)S(1)}, f32[2816,128]{1,0:T(8,128)S(1)}, f32[16,1,128]{2,1,0:T(1,128)S(1)}) custom-call(s32[64]{0:T(128)} %order_hbm.1, s32[2,128]{1,0:T(2,128)} %bitcast.7, f32[1,200]{1,0:T(1,128)} %bitcast.8, f32[8,800,512]{2,1,0:T(8,128)} %bitcast.5, f32[800,600]{1,0:T(8,128)} %w_hbm.1), custom_call_target="tpu_custom_call" | custom-call | flops 11796480000 | bytes 13107200 | tf_op jit(solution)/shard_map/exchange/pallas_call | solution.py:332
  218.4 3.8 %finish.1 = (f32[32,600,128]{2,1,0:T(8,128)}, f32[1,128]{1,0:T(1,128)}) custom-call(f32[24,600,128]{2,1,0:T(8,128)S(1)} %get-tuple-element.8.main_ref, f32[4,128,40,128]{3,2,1,0:T(8,128)S(1)} %get-tuple-element.9.recv_main, f32[2816,128]{1,0:T(8,128)S(1)} %get-tuple-element.10.rest_turned, f32[16,1,128]{2,1,0:T(1,128)S(1)} %get-tuple-element.11.sq_ref), custom_call_target="tpu_custom_call" | custom-call | tf_op jit(solution)/shard_map/finish/pallas_call | solution.py:375
